TPU v7x, 256 devices: a whole 4x4x8 slice. The times are simulated.
256 devices in a mesh: cluster: 64 (over x, z, core), dir: 4 (over y).
Axes of the slice: x: 4, y: 4, z: 8, core: 2. Of those that a mesh axis runs over, the one named last changes fastest.
Arguments:
- ray_code: int32 [1024, 524288], P('dir', 'cluster'), may hold values from 0 to 16, as said below
- occluder_list: int32 [64, 16], replicated, may hold values from 0 to 511, as said below
- list_count: int32 [64], replicated, may hold values from 1 to 16, 768 in all
- normal_azimuth: float32 [524288], P('cluster'), may hold values from -3.140625 to 3.140625
- normal_height: float32 [524288], P('cluster'), may hold values from -1 to 1
- albedo: float32 [524288], P('cluster'), may hold values from 0.2 to 1
- occluder_exit_radiance: bfloat16 [512, 81, 1024], P('cluster', None, 'dir'), may hold values from -18 to 18
Outputs:
- transfer: bfloat16 [81, 524288], P(None, ('cluster', 'dir'))
Inputs may be any that keep to these rules, and one draw needn't show every extreme that they name: `occluder_list`: each row names 16 different blocks, exactly 2 held by each of 8 different clusters; block b is held by cluster b // 8. `list_count`: entry c is the number of leading slots of row c of occluder_list in use. `ray_code`: A code of a vertex of cluster c below list_count[c] names the slot of that cluster's list whose block the ray ends on; any other code means the ray escapes.
All inputs are finite; a program needn't handle non-finite values.
Results may differ from a plain program's by a relative error of at most 0.0041.
Values may be sent and summed in bfloat16 or wider, within the bound.
A program may use at most 128 MiB of HBM per device.

v0:
```python
import math
import jax
import jax.numpy as jnp
from jax import lax
from jax.sharding import PartitionSpec as P

NDIR = 1024
SHORD = 9
golden_angle = math.pi * (3.0 - math.sqrt(5.0))


def sphere_points(direction_index, direction_overall_count):
    position = direction_index.astype(jnp.float32)
    along_z = 1.0 - (2.0 * position + 1.0) / direction_overall_count
    radius = jnp.sqrt(jnp.maximum(1.0 - along_z * along_z, 0.0))
    turned = position * golden_angle
    return (radius * jnp.cos(turned), radius * jnp.sin(turned), along_z)


def harmonic_table(along_x, along_y, along_z, degrees):
    cosine_terms = [jnp.ones_like(along_x)]
    sine_terms = [jnp.zeros_like(along_x)]
    for power_exponent in range(1, degrees):
        cosine_terms.append(cosine_terms[-1] * along_x - sine_terms[-1] * along_y)
        sine_terms.append(cosine_terms[-2] * along_y + sine_terms[-1] * along_x)
    basis_rows = [None] * (degrees * degrees)
    for order_index in range(degrees):
        diagonal_entries = 1.0
        for factor in range(1, 2 * order_index, 2):
            diagonal_entries = diagonal_entries * factor
        legendre = [None] * degrees
        legendre[order_index] = jnp.full_like(along_z, diagonal_entries)
        if order_index + 1 < degrees:
            legendre[order_index + 1] = along_z * ((2 * order_index + 1) * diagonal_entries)
        for degree in range(order_index + 2, degrees):
            legendre[degree] = (
                (2 * degree - 1) * along_z * legendre[degree - 1]
                - (degree + order_index - 1) * legendre[degree - 2]
            ) / (degree - order_index)
        for degree in range(order_index, degrees):
            factor_norm = math.sqrt(
                (2 * degree + 1)
                / (4.0 * math.pi)
                * math.factorial(degree - order_index)
                / math.factorial(degree + order_index)
            )
            centre = degree * degree + degree
            if order_index == 0:
                basis_rows[centre] = factor_norm * legendre[degree]
            else:
                basis_rows[centre + order_index] = (
                    math.sqrt(2.0) * factor_norm * legendre[degree] * cosine_terms[order_index]
                )
                basis_rows[centre - order_index] = (
                    math.sqrt(2.0) * factor_norm * legendre[degree] * sine_terms[order_index]
                )
    return jnp.stack(basis_rows)


def facing_table(normal_azimuth, normal_height, along_x, along_y, along_z):
    planar = jnp.sqrt(jnp.maximum(1.0 - normal_height * normal_height, 0.0))
    normal_x = planar * jnp.cos(normal_azimuth)
    normal_y = planar * jnp.sin(normal_azimuth)
    return jnp.maximum(
        along_x[:, None] * normal_x[None, :]
        + along_y[:, None] * normal_y[None, :]
        + along_z[:, None] * normal_height[None, :],
        0.0,
    )


def per_device(
    ray_code,
    occluder_list,
    list_count,
    normal_azimuth,
    normal_height,
    albedo,
    occluder_exit_radiance,
):
    dir_total, vertex_total = ray_code.shape
    blocks_held, coeff_total = (occluder_exit_radiance.shape[0], occluder_exit_radiance.shape[1])
    clusters, slot_total = occluder_list.shape
    own_cluster = lax.axis_index("cluster")
    first_dir = lax.axis_index("dir") * dir_total
    along_x, along_y, along_z = sphere_points(first_dir + lax.iota(jnp.int32, dir_total), NDIR)
    harmonics = harmonic_table(along_x, along_y, along_z, SHORD)
    facing = facing_table(normal_azimuth, normal_height, along_x, along_y, along_z)
    live_count = list_count[own_cluster]
    occluded = ray_code < live_count
    direct = jnp.dot(
        harmonics,
        jnp.where(occluded, 0.0, facing),
        precision=lax.Precision.HIGHEST,
        preferred_element_type=jnp.float32,
    )
    own_list = occluder_list[own_cluster]
    slot_index = lax.iota(jnp.int32, slot_total)
    portion_slice = lax.all_gather(occluder_exit_radiance, "cluster", axis=0, tiled=True)
    selected_entries = own_list[:, None] == lax.iota(jnp.int32, portion_slice.shape[0])[None, :]
    entries = jnp.einsum(
        "fx,xwn->fwn",
        selected_entries.astype(jnp.bfloat16),
        portion_slice,
        preferred_element_type=jnp.float32,
    ).astype(jnp.bfloat16)
    stacked = jnp.transpose(entries, (1, 0, 2)).reshape(coeff_total, slot_total * dir_total)
    block_width = min(512, vertex_total)
    block_count = vertex_total // block_width

    def one_block(block_index):
        first_vertex = block_index * block_width
        ray_codes = lax.dynamic_slice_in_dim(ray_code, first_vertex, block_width, 1)
        lit = lax.dynamic_slice_in_dim(facing, first_vertex, block_width, 1)
        weight = jnp.where(ray_codes < live_count, lit, 0.0)
        onehot = ray_codes[None, :, :] == slot_index[:, None, None]
        spread = (
            jnp.where(onehot, weight[None, :, :], 0.0)
            .astype(jnp.bfloat16)
            .reshape(slot_total * dir_total, block_width)
        )
        return jnp.dot(stacked, spread, preferred_element_type=jnp.float32)

    pieces = lax.map(one_block, lax.iota(jnp.int32, block_count))
    bounce = jnp.transpose(pieces, (1, 0, 2)).reshape(coeff_total, vertex_total)
    partial_sum = 4.0 * math.pi / NDIR * (direct + albedo[None, :] * bounce)
    summed = lax.psum_scatter(partial_sum, "dir", scatter_dimension=1, tiled=True)
    return summed.astype(jnp.bfloat16)


def solution(mesh):
    return jax.shard_map(
        per_device,
        mesh=mesh,
        in_specs=(
            P("dir", "cluster"),
            P(),
            P(),
            P("cluster"),
            P("cluster"),
            P("cluster"),
            P("cluster", None, "dir"),
        ),
        out_specs=P(None, ("cluster", "dir")),
        check_vma=False,
    )
```

profile of v0, /device:TPU:1, one launch (start us, length us, event | category | flops | bytes accessed | tf_op | source)
XLA Modules:
  0.0 316.4 jit_solution(9582630595501091377)
XLA Ops:
  12.7 4.3 %add_maximum_fusion = bf16[256,8192]{1,0:T(8,128)(2,1)} fusion(f32[8192]{0:T(1024)} %param.13, f32[256]{0:T(256)S(1)} %multiply_subtract_fusion, f32[8192]{0:T(1024)S(1)} %get-tuple-element.99, f32[256]{0:T(256)S(1)} %get-tuple-element.100, f32[8192]{0:T(1024)S(1)} %get-tuple-element.98, f32[256]{0:T(256)S(1)} %get-tuple-element.101), kind=kLoop, calls=%fused_computation.11 | loop fusion | flops 14680064 | bytes 4295680 | tf_op jit(solution)/shard_map/max | solution.py:64
  17.0 115.2 %all-gather.2.cloned.1.call-done = bf16[512,81,256]{2,0,1:T(8,128)(2,1)} async-done(((bf16[8,81,256]{2,0,1:T(8,128)(2,1)}), bf16[512,81,256]{2,0,1:T(8,128)(2,1)}) %all-gather.2.cloned.1.call-update) | async-done | bytes 21233680 | tf_op jit(solution)/shard_map/all_gather | solution.py:99
  132.1 10.0 %fusion.7 = bf16[81,16,256]{2,1,0:T(8,128)(2,1)S(1)} fusion(bf16[512,81,256]{2,0,1:T(8,128)(2,1)} %all-gather.2.cloned.1.call-done, s32[16]{0:T(128)S(1)} %dynamic-slice_reduce_fusion), kind=kOutput, calls=%fused_computation.16 | convolution fusion | flops 340078592 | bytes 21897280 | tf_op jit(solution)/shard_map/fx,xwn->fwn/dot_general | solution.py:101
  142.5 114.1 %while.12 = (s32[]{:T(128)}, f32[16,81,512]{2,1,0:T(8,128)}, s32[16]{0:T(128)S(1)}, s32[256,8192]{1,0:T(8,128)}, s32[]{:T(128)}, /*index=5*/bf16[256,8192]{1,0:T...) while((s32[]{:T(128)}, f32[16,81,512]{2,1,0:T(8,128)}, ...), condition=%wide.region_1.2_spmd.clone, body=%wide.region_0.1_spmd.clone.sunk | while | flops 344195072 | bytes 12181759 | solution.py:124
  143.8 1.8 dynamic-slice_select_fusion.2
  146.7 1.4 fusion.36
  148.1 1.5 fusion.37
  151.0 1.8 dynamic-slice_select_fusion.2
  153.8 1.4 fusion.36
  155.2 1.5 fusion.37
  158.1 1.8 dynamic-slice_select_fusion.2
  161.0 1.4 fusion.36
  162.4 1.5 fusion.37
  165.2 1.8 dynamic-slice_select_fusion.2
  168.1 1.4 fusion.36
  169.5 1.5 fusion.37
  172.4 1.8 dynamic-slice_select_fusion.2
  175.2 1.4 fusion.36
  176.6 1.5 fusion.37
  179.5 1.8 dynamic-slice_select_fusion.2
  182.4 1.4 fusion.36
  183.8 1.5 fusion.37
  186.6 1.8 dynamic-slice_select_fusion.2
  189.5 1.4 fusion.36
  190.9 1.5 fusion.37
  193.8 1.8 dynamic-slice_select_fusion.2
  198.0 1.5 fusion.37
  200.9 1.8 dynamic-slice_select_fusion.2
  205.2 1.5 fusion.37
  208.0 1.8 dynamic-slice_select_fusion.2
  212.3 1.5 fusion.37
  215.2 1.8 dynamic-slice_select_fusion.2
  219.4 1.5 fusion.37
  222.3 1.8 dynamic-slice_select_fusion.2
  226.6 1.5 fusion.37
  229.4 1.8 dynamic-slice_select_fusion.2
  233.7 1.5 fusion.37
  236.6 1.8 dynamic-slice_select_fusion.2
  240.8 1.5 fusion.37
  243.7 1.8 dynamic-slice_select_fusion.2
  248.0 1.5 fusion.37
  250.8 1.8 dynamic-slice_select_fusion.2
  255.1 1.5 fusion.37
  256.6 3.5 %copy.9 = f32[81,16,512]{2,1,0:T(8,128)S(1)} copy(f32[81,16,512]{2,0,1:T(8,128)} %bitcast.55) | data formatting | bytes 5308416 | tf_op jit(solution)/shard_map/transpose | solution.py:125
  260.6 2.0 copy.12
  262.7 9.5 %fusion.2 = f32[81,8192]{1,0:T(8,128)} fusion(f32[81,256]{1,0:T(8,128)S(1)} %stack.5, s32[256,8192]{1,0:T(8,128)S(1)} %bitcast.54, s32[]{:T(128)} %bitcast, f32[81,8192]{1,0:T(8,128)S(1)} %bitcast.56, f32[8192]{0:T(1024)S(1)} %copy-done.2, f32[8192]{0:T(1024)S(1)} %copy-done.1, f32[256]{0:T(256)S(1)} %multiply_subtract_fusion, ...), kind=kOutput, calls=%fused_computation.9 | convolution fusion | flops 2057199616 | bytes 13914116 | tf_op jit(solution)/shard_map/dot_general | solution.py:91
  272.2 35.5 %reduce-scatter.2.cloned.1.call-done = f32[81,2048]{1,0:T(8,128)} async-done(((f32[81,8192]{1,0:T(8,128)}), f32[81,2048]{1,0:T(8,128)}) %reduce-scatter.2.cloned.1.call-update) | async-done | bytes 663568 | tf_op jit(solution)/shard_map/reduce_scatter | solution.py:127
  307.7 1.9 convert_element_type.358
  (140 shorter events, 48.5 us)
Async XLA Ops:
  6.5 5.0 %copy-start = (s32[64,16]{0,1:T(8,128)S(1)}, s32[64,16]{0,1:T(8,128)}, u32[]{:S(2)}) copy-start(s32[64,16]{0,1:T(8,128)} %param.10) | copy-start | bytes 12292
  6.5 125.6 %all-gather.2.cloned.1.call-start = ((), (), s32[]{:S(2)}) async-start(), calls=%async_computation.1 | async-start | bytes 21565440 | tf_op jit(solution)/shard_map/all_gather | solution.py:99
  7.3 300.4 %reduce-scatter.2.cloned.1.call-start = ((), (), s32[]{:S(2)}) async-start(), calls=%async_computation.2 | async-start | bytes 3604480 | tf_op jit(solution)/shard_map/reduce_scatter | solution.py:127
  256.6 6.0 %slice-start = ((s8[8388608]{0:T(1024)(128)(4,1)}), s8[4194304]{0:T(1024)(128)(4,1)S(1)}, s32[]{:S(2)}) async-start(s8[8388608]{0:T(1024)(128)(4,1)} %bitcast.53), calls=%async_computation.3 | async-start | bytes 8388608
  256.6 6.0 %copy-start.1 = (f32[8192]{0:T(1024)S(1)}, f32[8192]{0:T(1024)}, u32[]{:S(2)}) copy-start(f32[8192]{0:T(1024)} %param.13) | copy-start | bytes 98308
  256.6 6.0 %copy-start.2 = (f32[8192]{0:T(1024)S(1)}, f32[8192]{0:T(1024)}, u32[]{:S(2)}) copy-start(f32[8192]{0:T(1024)} %param.14) | copy-start | bytes 98308
  260.1 2.5 slice-start.1
Sparse Core Ops, SparseCore 0:
  9.9 122.2 all-gather.1
  272.3 35.2 reduce-scatter.1
where the time goes:
time: 318 us; the launch traced here: 316 us
  waiting for transfers between devices  151 us (47%)
  other arithmetic  60.5 us (19%)
  matrix products  43.5 us (14%)
  local copies, waits for them, and re-layouts  37 us (12%)
  between operations  13.6 us (4%)
  loops' own time  10.4 us (3%)
    all_gather x1, waiting for transfers between devices, per_device(): lax.all_gather(occluder_exit_radiance, 'cluster', axis=0, tiled=True)  115 us
    reduce_scatter x1, waiting for transfers between devices, per_device(): lax.psum_scatter(partial_sum, 'dir', scatter_dimension=1, tiled=True)  35.5 us
    select_n x16, other arithmetic, one_block(): weight = jnp.where(ray_codes < live_count, lit, 0.0)  28.3 us
    dot_general x16, matrix products, one_block(): return jnp.dot(stacked, spread, preferred_element_type=jnp.float32)  24.1 us
    convert_element_type x16, other arithmetic, one_block(): spread = jnp.where(onehot, weight[None, :, :], 0.0).astype(jnp.bfloat16)....  22.4 us
    dynamic_slice x16, local copies, waits for them, and re-layouts, one_block(): ray_codes = lax.dynamic_slice_in_dim(ray_code, first_vertex, block_width, 1)  17.3 us
    another operation x1, loops' own time, per_device(): pieces = lax.map(one_block, lax.iota(jnp.int32, block_count))  10.4 us
    dynamic_slice x16, local copies, waits for them, and re-layouts, per_device(): pieces = lax.map(one_block, lax.iota(jnp.int32, block_count))  10.3 us
  transfers between devices with their start and end apart: 2, of which 2 were waited for; matrix products, arithmetic and copies ran while one was open for 3% of the time, Pallas kernels for 0%

commit v1 on v0

--- a/solution.py
+++ b/solution.py
@@ -96,7 +96,8 @@
     )
     own_list = occluder_list[own_cluster]
     slot_index = lax.iota(jnp.int32, slot_total)
-    portion_slice = lax.all_gather(occluder_exit_radiance, "cluster", axis=0, tiled=True)
+    copies = jnp.concatenate([occluder_exit_radiance] * lax.axis_size("cluster"), axis=0)
+    portion_slice = lax.all_to_all(copies, "cluster", 0, 0, tiled=True)
     selected_entries = own_list[:, None] == lax.iota(jnp.int32, portion_slice.shape[0])[None, :]
     entries = jnp.einsum(
         "fx,xwn->fwn",

time: 318 us -> 800 us (2.52)
  waiting for transfers between devices: 151 us -> 530 us
  local copies, waits for them, and re-layouts: 37 us -> 119 us
  starting transfers between devices: 0.04 us -> 13.5 us
    all_to_all x0 -> x1, waiting for transfers between devices: none -> 493 us  [per_device(): portion_slice = lax.all_to_all(copies, 'cluster', 0, 0, tiled=True)]
    all_gather x1 -> x0, waiting for transfers between devices: 115 us -> none  [per_device(): lax.all_gather(occluder_exit_radiance, 'cluster', axis=0, tiled=True)]
    unnamed x14 -> x81, local copies, waits for them, and re-layouts: 2.81 us -> 85.9 us
    all_to_all x0 -> x1, starting transfers between devices: none -> 13.3 us  [per_device(): portion_slice = lax.all_to_all(copies, 'cluster', 0, 0, tiled=True)]
  transfers between devices with their start and end apart: 2 -> 2, of which waited for: 2 -> 2; matrix products, arithmetic and copies ran while one was open for 3% -> 1% of each run, Pallas kernels for 0% -> 0%
where the time goes in v1:
time: 800 us; the launch traced here: 797 us
  waiting for transfers between devices  530 us (66%)
  local copies, waits for them, and re-layouts  119 us (15%)
  other arithmetic  60 us (8%)
  matrix products  49.9 us (6%)
  between operations  13.6 us (2%)
  starting transfers between devices  13.5 us (2%)
  loops' own time  10.6 us (1%)
    all_to_all x1, waiting for transfers between devices, per_device(): portion_slice = lax.all_to_all(copies, 'cluster', 0, 0, tiled=True)  493 us
    unnamed x81, local copies, waits for them, and re-layouts  85.9 us
    reduce_scatter x1, waiting for transfers between devices, per_device(): lax.psum_scatter(partial_sum, 'dir', scatter_dimension=1, tiled=True)  37.2 us
    select_n x16, other arithmetic, one_block(): weight = jnp.where(ray_codes < live_count, lit, 0.0)  29.3 us
    dot_general x16, matrix products, one_block(): return jnp.dot(stacked, spread, preferred_element_type=jnp.float32)  24.1 us
    convert_element_type x16, other arithmetic, one_block(): spread = jnp.where(onehot, weight[None, :, :], 0.0).astype(jnp.bfloat16)....  22.4 us
    dynamic_slice x16, local copies, waits for them, and re-layouts, one_block(): ray_codes = lax.dynamic_slice_in_dim(ray_code, first_vertex, block_width, 1)  17.3 us
  transfers between devices with their start and end apart: 2, of which 2 were waited for; matrix products, arithmetic and copies ran while one was open for 1% of the time, Pallas kernels for 0%

profile of v1, /device:TPU:1, one launch (start us, length us, event | category | flops | bytes accessed | tf_op | source)
XLA Modules:
  0.0 797.1 jit_solution(16762627675640138851)
XLA Ops:
  6.5 1.9 constant_dynamic-update-slice_fusion.63
  10.2 1.8 constant_dynamic-update-slice_fusion.61
  11.9 1.8 constant_dynamic-update-slice_fusion.60
  13.8 1.8 constant_dynamic-update-slice_fusion.59
  15.6 1.8 constant_dynamic-update-slice_fusion.58
  17.4 1.8 constant_dynamic-update-slice_fusion.57
  20.9 1.8 constant_dynamic-update-slice_fusion.55
  22.7 1.8 constant_dynamic-update-slice_fusion.54
  24.5 1.8 constant_dynamic-update-slice_fusion.53
  26.3 1.8 constant_dynamic-update-slice_fusion.52
  33.4 1.8 constant_dynamic-update-slice_fusion.48
  35.2 1.8 constant_dynamic-update-slice_fusion.47
  37.0 1.8 constant_dynamic-update-slice_fusion.46
  40.6 1.8 constant_dynamic-update-slice_fusion.44
  42.3 1.8 constant_dynamic-update-slice_fusion.43
  44.1 1.8 constant_dynamic-update-slice_fusion.42
  49.5 1.8 constant_dynamic-update-slice_fusion.39
  51.2 1.8 constant_dynamic-update-slice_fusion.38
  54.8 1.8 constant_dynamic-update-slice_fusion.36
  58.4 1.8 constant_dynamic-update-slice_fusion.34
  60.1 1.8 constant_dynamic-update-slice_fusion.33
  61.9 1.8 constant_dynamic-update-slice_fusion.32
  90.5 13.3 %all-to-all-start = ((bf16[512,81,256]{2,1,0:T(8,128)(2,1)}), bf16[512,81,256]{2,1,0:T(8,128)(2,1)}, u32[]{:S(2)}, u32[]{:S(2)}) async-start(bf16[512,81,256]{2,1,0:T(8,128)(2,1)} %constant_dynamic-update-slice_fusion), calls=%async_computation | async-start | bytes 46137344 | tf_op jit(solution)/shard_map/all_to_all | solution.py:100
  108.0 3.5 add_maximum_fusion
  111.5 492.7 %all-to-all-done = bf16[512,81,256]{2,1,0:T(8,128)(2,1)} async-done(((bf16[512,81,256]{2,1,0:T(8,128)(2,1)}), bf16[512,81,256]{2,1,0:T(8,128)(2,1)}, u32[]{:S(2)}, u32[]{:S(2)}) %all-to-all-start) | async-done | bytes 21233696 | tf_op jit(solution)/shard_map/all_to_all | solution.py:100
  604.2 12.9 %fusion.12 = bf16[81,16,256]{2,1,0:T(8,128)(2,1)S(1)} fusion(bf16[512,81,256]{2,1,0:T(8,128)(2,1)} %all-to-all-done, s32[16]{0:T(128)S(1)} %dynamic-slice_reduce_fusion), kind=kOutput, calls=%fused_computation.18 | convolution fusion | flops 340078592 | bytes 21897280 | tf_op jit(solution)/shard_map/fx,xwn->fwn/dot_general | solution.py:102
  617.5 114.8 %while.12 = (s32[]{:T(128)}, f32[16,81,512]{2,1,0:T(8,128)}, s32[16]{0:T(128)S(1)}, s32[256,8192]{1,0:T(8,128)}, s32[]{:T(128)}, /*index=5*/bf16[256,8192]{1,0:T...) while((s32[]{:T(128)}, f32[16,81,512]{2,1,0:T(8,128)}, ...), condition=%wide.region_1.2_spmd.clone, body=%wide.region_0.1_spmd.clone.sunk | while | flops 344195072 | bytes 12182259 | solution.py:125
  618.7 1.8 dynamic-slice_select_fusion.2
  625.9 1.8 dynamic-slice_select_fusion.2
  633.1 1.8 dynamic-slice_select_fusion.2
  640.3 1.8 dynamic-slice_select_fusion.2
  647.4 1.8 dynamic-slice_select_fusion.2
  654.6 1.8 dynamic-slice_select_fusion.2
  661.8 1.8 dynamic-slice_select_fusion.2
  668.9 1.8 dynamic-slice_select_fusion.2
  676.1 1.8 dynamic-slice_select_fusion.2
  683.3 1.8 dynamic-slice_select_fusion.2
  690.5 1.8 dynamic-slice_select_fusion.2
  697.6 1.8 dynamic-slice_select_fusion.2
  704.8 1.8 dynamic-slice_select_fusion.2
  712.0 1.8 dynamic-slice_select_fusion.2
  719.1 1.8 dynamic-slice_select_fusion.2
  726.3 1.8 dynamic-slice_select_fusion.2
  732.2 3.4 copy.75
  736.1 2.0 copy.78
  738.1 13.0 %fusion.4 = f32[81,8192]{1,0:T(8,128)} fusion(f32[81,256]{1,0:T(8,128)S(1)} %stack.5, s32[256,8192]{1,0:T(8,128)} %get-tuple-element.259, s32[]{:T(128)} %bitcast, f32[81,8192]{1,0:T(8,128)S(1)} %bitcast.53, f32[8192]{0:T(1024)S(1)} %copy-done.5, f32[8192]{0:T(1024)S(1)} %copy-done.3, f32[256]{0:T(256)S(1)} %multiply_subtract_fusion, ...), kind=kOutput, calls=%fused_computation.11 | convolution fusion | flops 2057199616 | bytes 13914116 | tf_op jit(solution)/shard_map/dot_general | solution.py:91
  751.1 37.2 %reduce-scatter.2.cloned.1.call-done = f32[81,2048]{1,0:T(8,128)} async-done(((f32[81,8192]{1,0:T(8,128)}), f32[81,2048]{1,0:T(8,128)}) %reduce-scatter.2.cloned.1.call-update) | async-done | bytes 663568 | tf_op jit(solution)/shard_map/reduce_scatter | solution.py:128
  788.3 1.9 convert_element_type.358
  (206 shorter events, 124.3 us)
Async XLA Ops:
  6.5 101.1 %copy-start = (s32[64,16]{0,1:T(8,128)S(1)}, s32[64,16]{0,1:T(8,128)}, u32[]{:S(2)}) copy-start(s32[64,16]{0,1:T(8,128)} %param.10) | copy-start | bytes 12292
  6.5 58.9 %copy-start.2 = (bf16[8,81,256]{2,0,1:T(8,128)(2,1)S(1)}, bf16[8,81,256]{2,0,1:T(8,128)(2,1)}, u32[]{:S(2)}) copy-start(bf16[8,81,256]{2,0,1:T(8,128)(2,1)} %param.15) | copy-start | bytes 995332
  90.5 13.5 %copy-start.6 = (s32[64]{0:T(128)S(1)}, s32[64]{0:T(128)}, u32[]{:S(2)}) copy-start(s32[64]{0:T(128)} %param.11) | copy-start | bytes 772
  90.5 17.4 %copy-start.3 = (f32[8192]{0:T(1024)S(1)}, f32[8192]{0:T(1024)}, u32[]{:S(2)}) copy-start(f32[8192]{0:T(1024)} %param.13) | copy-start | bytes 98308
  90.5 17.4 %copy-start.4 = (f32[8192]{0:T(1024)S(1)}, f32[8192]{0:T(1024)}, u32[]{:S(2)}) copy-start(f32[8192]{0:T(1024)} %param.12) | copy-start | bytes 98308
  90.5 513.8 %all-to-all-start = ((bf16[512,81,256]{2,1,0:T(8,128)(2,1)}), bf16[512,81,256]{2,1,0:T(8,128)(2,1)}, u32[]{:S(2)}, u32[]{:S(2)}) async-start(bf16[512,81,256]{2,1,0:T(8,128)(2,1)} %constant_dynamic-update-slice_fusion), calls=%async_computation | async-start | bytes 46137344 | tf_op jit(solution)/shard_map/all_to_all | solution.py:100
  103.8 684.6 %reduce-scatter.2.cloned.1.call-start = ((), (), s32[]{:S(2)}) async-start(), calls=%async_computation.2 | async-start | bytes 3604480 | tf_op jit(solution)/shard_map/reduce_scatter | solution.py:128
  617.4 120.6 %copy-start.5 = (f32[8192]{0:T(1024)S(1)}, f32[8192]{0:T(1024)}, u32[]{:S(2)}) copy-start(f32[8192]{0:T(1024)} %param.14) | copy-start | bytes 98308
  732.2 58.0 %copy-start.1 = (s32[64,16]{0,1:T(8,128)S(1)}, s32[64,16]{0,1:T(8,128)}, u32[]{:S(2)}) copy-start(s32[64,16]{0,1:T(8,128)} %param.10) | copy-start | bytes 12292
Sparse Core Ops, SparseCore 0:
  751.2 37.0 reduce-scatter.1
